TPU v7x, 32 devices: a whole 2x2x4 slice. The times are simulated.
32 devices in a mesh: seq: 16 (over z, y, x), tp: 2 (over core).
Axes of the slice: x: 2, y: 2, z: 4, core: 2. Of those that a mesh axis runs over, the one named last changes fastest.
Arguments:
- tokens: bfloat16 [8192, 2048], P('seq', 'tp'), may hold values from -6 to 6
- ln_gain: bfloat16 [2048], replicated, may hold values from 0.5 to 4.1
- w_qkv: bfloat16 [3, 2048, 2048], P(None, None, 'tp'), may hold values from -0.15467961 to 0.15467961
- w_out: bfloat16 [2048, 2048], P('tp'), may hold values from -0.1875 to 0.1875
Outputs:
- mixed: bfloat16 [8192, 2048], P('seq', 'tp')
All inputs are finite; a program needn't handle non-finite values.
Results may differ from a plain program's by a relative error of at most 0.011.
Values may be sent and summed in bfloat16 or wider, within the bound.
A program may use at most 256 MiB of HBM per device.

v0:
```python
import jax
import jax.numpy as jnp
from jax import lax
from jax.sharding import PartitionSpec as P

HEAD_DIM = 128


def attend_block(totals, queries, block_kv, factor):
    running, denoms, accum = totals
    heads_here = queries.shape[1]
    keys_part = block_kv[0].reshape(block_kv.shape[1], heads_here, queries.shape[2])
    vals_part = block_kv[1].reshape(block_kv.shape[1], heads_here, queries.shape[2])
    scores = (
        jnp.einsum("thc,shc->ths", queries, keys_part, preferred_element_type=jnp.float32) * factor
    )
    highest = jnp.maximum(running, jnp.max(scores, axis=2))
    expon = jnp.exp(scores - highest[:, :, None])
    denoms = jnp.sum(expon, axis=2)
    weights = expon.astype(jnp.bfloat16)
    accum = jnp.einsum("ths,shc->thc", weights, vals_part, preferred_element_type=jnp.float32)
    return (highest, denoms, accum)


def start_totals(rows, heads_count):
    return (
        jnp.full((rows, heads_count), -1e30, jnp.float32),
        jnp.zeros((rows, heads_count), jnp.float32),
        jnp.zeros((rows, heads_count, HEAD_DIM), jnp.float32),
    )


def on_device(tokens, ln_gain, w_qkv, w_out):
    tok_rows = tokens.shape[0]
    whole = lax.all_gather(tokens, "tp", axis=1, tiled=True)
    values = whole.astype(jnp.float32)
    average = jnp.mean(values, axis=1, keepdims=True)
    second = jnp.mean(values * values, axis=1, keepdims=True)
    normed = (
        (values - average)
        * lax.rsqrt(second - average * average + 1e-06)
        * ln_gain.astype(jnp.float32)
    ).astype(jnp.bfloat16)
    projected = jnp.einsum("td,jdc->jtc", normed, w_qkv, preferred_element_type=jnp.float32).astype(
        jnp.bfloat16
    )
    heads_here = w_qkv.shape[2] // HEAD_DIM
    factor = HEAD_DIM ** (-0.5)
    queries = projected[0].reshape(tok_rows, heads_here, HEAD_DIM)
    keys_vals = projected[1:3]
    initial = start_totals(tok_rows, heads_here)
    final = attend_block(
        initial, queries, lax.all_gather(keys_vals, "seq", axis=1, tiled=True), factor
    )
    context = (
        (final[2] / final[1][:, :, None])
        .reshape(tok_rows, heads_here * HEAD_DIM)
        .astype(jnp.bfloat16)
    )
    summed = lax.psum_scatter(
        lax.dot_general(
            w_out, context, (((0,), (1,)), ((), ())), preferred_element_type=jnp.float32
        ).astype(jnp.bfloat16),
        "tp",
        scatter_dimension=0,
        tiled=True,
    ).astype(jnp.float32)
    return (tokens.astype(jnp.float32) + summed.T).astype(jnp.bfloat16)


def solution(mesh):
    in_specs = (P("seq", "tp"), P(), P(None, None, "tp"), P("tp", None))
    out_specs = P("seq", "tp")
    return jax.shard_map(
        on_device, mesh=mesh, in_specs=in_specs, out_specs=out_specs, check_vma=False
    )
```

profile of v0, /device:TPU:15, one launch (start us, length us, event | category | flops | bytes accessed | tf_op | source)
XLA Modules:
  0.0 598.9 jit_solution(8259866064880003707)
XLA Ops:
  6.5 0.7 all-gather.3.cloned.1.call-update
  7.3 0.0 all-gather.5.cloned.1.call-start
  7.3 0.7 convert_element_type.39
  8.0 13.3 %all-gather.3.cloned.1.call-done = bf16[512,2048]{1,0:T(8,128)(2,1)} async-done(((bf16[512,1024]{1,0:T(8,128)(2,1)}), bf16[512,2048]{1,0:T(8,128)(2,1)}) %all-gather.3.cloned.1.call-update) | async-done | bytes 2097168 | tf_op jit(solution)/shard_map/all_gather | solution.py:35
  21.3 2.3 convert_reduce_fusion
  23.6 10.5 %convert_bitcast_fusion = bf16[3,512,1024]{2,1,0:T(8,128)(2,1)S(1)} fusion(bf16[3,2048,1024]{2,1,0:T(8,128)(2,1)} %param.6, bf16[512,2048]{1,0:T(8,128)(2,1)} %all-gather.3.cloned.1.call-done, f32[2048]{0:T(1024)S(1)} %convert_element_type.39, f32[512]{0:T(512)S(1)} %get-tuple-element.10, f32[512]{0:T(512)S(1)} %get-tuple-element.9), kind=kOutput, calls=%fused_computation.16 | convolution fusion | flops 6449266688 | bytes 17838080 | tf_op jit(solution)/shard_map/td,jdc->jtc/dot_general | solution.py:44
  34.1 1.5 slice.16
  35.6 0.0 all-gather.5.cloned.1.call-update
  35.6 0.2 reduce-scatter.2.cloned.1.call-start
  35.8 0.1 slice_bitcast_fusion.1
  35.9 0.3 copy.12
  36.2 346.7 %all-gather.5.cloned.1.call-done = bf16[2,8192,1024]{2,1,0:T(8,128)(2,1)} async-done(((bf16[2,512,1024]{2,1,0:T(8,128)(2,1)}), bf16[2,8192,1024]{2,1,0:T(8,128)(2,1)}) %all-gather.5.cloned.1.call-update) | async-done | bytes 33554448 | tf_op jit(solution)/shard_map/all_gather | solution.py:53
  382.9 19.2 %slice_bitcast_fusion = (bf16[1024,8,8,128]{3,1,2,0:T(8,128)(2,1)S(1)}, bf16[1,8192,1024]{2,1,0:T(8,128)(2,1)}) fusion(bf16[2,8192,1024]{2,1,0:T(8,128)(2,1)} %all-gather.5.cloned.1.call-done), kind=kLoop, calls=%fused_computation.6 | loop fusion | bytes 67108864
  402.1 9.1 %copy.11 = bf16[1024,8,8,128]{3,2,1,0:T(8,128)(2,1)} copy(bf16[1024,8,8,128]{3,1,2,0:T(8,128)(2,1)S(1)} %get-tuple-element.7) | data formatting | bytes 33554432
  411.2 20.7 %copy.10 = bf16[1,8192,1024]{1,2,0:T(8,128)(2,1)} copy(bf16[1,8192,1024]{2,1,0:T(8,128)(2,1)} %get-tuple-element.8) | data formatting | bytes 33554432 | tf_op jit(solution)/shard_map/reshape;squeeze | solution.py:13
  431.9 50.1 %bitcast_reduce_fusion = (f32[512,8]{0,1:T(8,128)S(1)}, f32[8,8192,512]{2,1,0:T(8,128)}) fusion(bf16[512,8,128]{2,1,0:T(8,128)(2,1)S(1)} %bitcast.43, bf16[8192,8,128]{2,1,0:T(8,128)(2,1)} %bitcast.41), kind=kOutput, calls=%fused_computation.1 | convolution fusion | flops 8657039360 | bytes 152059904 | tf_op jit(solution)/shard_map/thc,shc->ths/dot_general | solution.py:15
  482.0 41.4 %fusion.1 = f32[512,8]{0,1:T(8,128)S(1)} fusion(f32[8,8192,512]{2,1,0:T(8,128)} %get-tuple-element.12, f32[512,8]{0,1:T(8,128)S(1)} %broadcast_maximum_fusion), kind=kLoop, calls=%fused_computation.3 | loop fusion | flops 100659200 | bytes 134250496 | tf_op jit(solution)/shard_map/reduce_sum | solution.py:19
  523.4 48.2 %fusion.15 = bf16[512,8,128]{0,2,1:T(8,128)(2,1)S(1)} fusion(bf16[8192,8,128]{0,2,1:T(8,128)(2,1)} %bitcast.42, f32[8,8192,512]{2,1,0:T(8,128)} %get-tuple-element.12, f32[512,8]{0,1:T(8,128)S(1)} %broadcast_maximum_fusion, f32[512,8]{0,1:T(8,128)S(1)} %fusion.1), kind=kOutput, calls=%fused_computation.23 | convolution fusion | flops 8691646464 | bytes 152076288 | tf_op jit(solution)/shard_map/ths,shc->thc/dot_general | solution.py:21
  571.6 0.0 copy-start
  571.6 6.0 %fusion.11 = bf16[2048,512]{0,1:T(8,128)(2,1)} fusion(bf16[512,1024]{0,1:T(8,128)(2,1)S(1)} %bitcast.44, bf16[1024,2048]{1,0:T(8,128)(2,1)} %param.7), kind=kOutput, calls=%fused_computation.18 | convolution fusion | flops 2148532224 | bytes 7340032 | tf_op jit(solution)/shard_map/dot_general | solution.py:61
  577.6 0.0 reduce-scatter.2.cloned.1.call-update
  577.6 12.1 %reduce-scatter.2.cloned.1.call-done = bf16[1024,512]{0,1:T(8,128)(2,1)} async-done(((bf16[2048,512]{0,1:T(8,128)(2,1)}), bf16[1024,512]{0,1:T(8,128)(2,1)}) %reduce-scatter.2.cloned.1.call-update) | async-done | bytes 1048592 | tf_op jit(solution)/shard_map/reduce_scatter | solution.py:60
  589.8 0.0 copy-done
  589.8 2.6 fusion.14
  (3 shorter events, 0.0 us)
Async XLA Ops:
  6.5 14.8 %all-gather.3.cloned.1.call-start = ((), (), s32[]{:S(2)}) async-start(), calls=%async_computation.1 | async-start | bytes 3145728 | tf_op jit(solution)/shard_map/all_gather | solution.py:35
  7.3 375.6 %all-gather.5.cloned.1.call-start = ((), (), s32[]{:S(2)}) async-start(), calls=%async_computation.2 | async-start | bytes 35651584 | tf_op jit(solution)/shard_map/all_gather | solution.py:53
  35.6 554.2 %reduce-scatter.2.cloned.1.call-start = ((), (), s32[]{:S(2)}) async-start(), calls=%async_computation.3 | async-start | bytes 3145728 | tf_op jit(solution)/shard_map/reduce_scatter | solution.py:60
  571.6 18.2 %copy-start = (bf16[512,1024]{1,0:T(8,128)(2,1)S(1)}, bf16[512,1024]{1,0:T(8,128)(2,1)}, u32[]{:S(2)}) copy-start(bf16[512,1024]{1,0:T(8,128)(2,1)} %param.4) | copy-start | bytes 3145732
Sparse Core Ops, SparseCore 0:
  8.9 12.3 all-gather.2
  35.7 347.0 all-gather.4
  577.8 11.9 reduce-scatter.1
where the time goes:
time: 601 us; the launch traced here: 599 us
  waiting for transfers between devices  373 us (62%)
  matrix products  115 us (19%)
  local copies, waits for them, and re-layouts  50.9 us (8%)
  other arithmetic  47 us (8%)
  between operations  13.2 us (2%)
    all_gather x1, waiting for transfers between devices, on_device(): lax.all_gather(keys_vals, 'seq', axis=1, tiled=True)  347 us
    dot_general x1, matrix products, attend_block(): jnp.einsum('thc,shc->ths', queries, keys_part, preferred_element_type=jnp...  50.1 us
    dot_general x1, matrix products, attend_block(): jnp.einsum('ths,shc->thc', weights, vals_part, preferred_element_type=jnp...  48.2 us
    reduce_sum x1, other arithmetic, attend_block(): denoms = jnp.sum(expon, axis=2)  41.4 us
    unnamed x6, local copies, waits for them, and re-layouts  28.7 us
    another operation x1, local copies, waits for them, and re-layouts, attend_block(): block_kv[1].reshape(block_kv.shape[1], heads_here, queries.shape[2])  20.7 us
    all_gather x1, waiting for transfers between devices, on_device(): whole = lax.all_gather(tokens, 'tp', axis=1, tiled=True)  13.3 us
    reduce_scatter x1, waiting for transfers between devices, on_device(): lax.psum_scatter(lax.dot_general(w_out, context, (((0,), (1,)), ((), ()))...  12.1 us
  transfers between devices with their start and end apart: 3, of which 3 were waited for; matrix products, arithmetic and copies ran while one was open for 0% of the time, Pallas kernels for 0%

commit v1 on v0

--- a/solution.py
+++ b/solution.py
@@ -1,9 +1,340 @@
+import functools
+import math
+
 import jax
 import jax.numpy as jnp
 from jax import lax
+from jax.experimental import pallas as pl
+from jax.experimental.pallas import tpu as pltpu
 from jax.sharding import PartitionSpec as P
 
 HEAD_DIM = 128
+MESH = pl.DeviceIdType.MESH
+ANY = pl.BlockSpec(memory_space=pl.ANY)
+
+
+def remote(src, dst, send, recv, seq, tp):
+    return pltpu.make_async_remote_copy(
+        src_ref=src, dst_ref=dst, send_sem=send, recv_sem=recv, device_id=(seq, tp), device_id_type=MESH
+    )
+
+
+def put(src, dst, send, recv, seq, tp, own):
+    @pl.when(own)
+    def _():
+        pltpu.make_async_copy(src, dst, recv).start()
+
+    @pl.when(jnp.logical_not(own))
+    def _():
+        remote(src, dst, send, recv, seq, tp).start()
+
+
+def project_kernel(
+    n, heads, tok, gain, w, q_out, kv_out,
+    pair, normed, wbuf, xq, xkv, wsem, psem, qsend, kvsend, qrecv, kvrecv, fsend, frecv,
+):
+    me, core = lax.axis_index("seq"), lax.axis_index("tp")
+    other = 1 - core
+    rows, feats = tok.shape
+    half = rows // 2
+    blocks = heads // 2
+    width = 2 * HEAD_DIM
+
+    mine = pltpu.make_async_copy(tok, pair.at[core], psem.at[0])
+    mine.start()
+    swap = remote(tok, pair.at[core], psem.at[1], psem.at[2], me, other)
+    swap.start()
+
+    def wcopy(b, j):
+        return pltpu.make_async_copy(w.at[j, :, pl.ds(pl.multiple_of(b * width, width), width)], wbuf.at[b, j], wsem.at[b, j])
+
+    def fetch(b, carry):
+        for j in range(3):
+            wcopy(b, j).start()
+        return carry
+
+    lax.fori_loop(0, blocks, fetch, 0)
+    mine.wait()
+    swap.wait()
+
+    step = 32
+
+    def norm(i, carry):
+        at = pl.ds(pl.multiple_of(i * step, step), step)
+        a = pair[0, at, :].astype(jnp.float32)
+        b = pair[1, at, :].astype(jnp.float32)
+        average = (jnp.sum(a, axis=1, keepdims=True) + jnp.sum(b, axis=1, keepdims=True)) / (2 * feats)
+        second = (jnp.sum(a * a, axis=1, keepdims=True) + jnp.sum(b * b, axis=1, keepdims=True)) / (2 * feats)
+        scale = lax.rsqrt(second - average * average + 1e-06)
+        normed[at, :feats] = ((a - average) * scale * gain[0:1, :feats]).astype(jnp.bfloat16)
+        normed[at, feats:] = ((b - average) * scale * gain[0:1, feats:]).astype(jnp.bfloat16)
+        return carry
+
+    lax.fori_loop(0, rows // step, norm, 0)
+
+    def sends(h, wait):
+        chip = core * heads + h
+        for u in range(2):
+            own = jnp.logical_and(chip == me, core == u)
+            at = pl.ds(u * half, half)
+            args_q = (xq.at[h, at], q_out.at[me], qsend.at[h, u], qrecv.at[me], chip, u)
+            args_kv = (xkv.at[h, at], kv_out.at[u, me], kvsend.at[h, u], kvrecv.at[me], chip, u)
+            if wait:
+
+                @pl.when(jnp.logical_not(own))
+                def _():
+                    remote(*args_q).wait_send()
+                    remote(*args_kv).wait_send()
+            else:
+                put(*args_kv, own)
+                put(*args_q, own)
+
+    factor = HEAD_DIM ** (-0.5) * math.log2(math.e)
+
+    def project(b, carry):
+        for j in range(3):
+            wcopy(b, j).wait()
+            got = jnp.dot(normed[...], wbuf[b, j], preferred_element_type=jnp.float32)
+            if j == 0:
+                got = got * factor
+            got = got.astype(jnp.bfloat16)
+            for i in range(2):
+                part = got[:, i * HEAD_DIM : (i + 1) * HEAD_DIM]
+                if j == 0:
+                    xq[2 * b + i] = part
+                else:
+                    xkv[2 * b + i, :, (j - 1) * HEAD_DIM : j * HEAD_DIM] = part
+
+        @pl.when(b > 0)
+        def _():
+            sends(2 * b - 2, False)
+            sends(2 * b - 1, False)
+
+        return carry
+
+    lax.fori_loop(0, blocks, project, 0)
+    sends(2 * blocks - 2, False)
+    sends(2 * blocks - 1, False)
+
+    def got_kv(s):
+        return remote(xkv.at[0, pl.ds(0, half)], kv_out.at[core, s], kvsend.at[0, 0], kvrecv.at[s], me, other)
+
+    def forward(s):
+        return remote(kv_out.at[core, s], kv_out.at[core, s], fsend.at[s], frecv.at[s], me, other)
+
+    def pass_on(i, carry):
+        s = lax.rem(me + i, n)
+        got_kv(s).wait_recv()
+        forward(s).start()
+        return carry
+
+    lax.fori_loop(0, n, pass_on, 0)
+
+    def finish(s, carry):
+        remote(xq.at[0, pl.ds(0, half)], q_out.at[s], qsend.at[0, 0], qrecv.at[s], me, other).wait_recv()
+        forward(s).wait_send()
+        remote(kv_out.at[other, s], kv_out.at[other, s], fsend.at[s], frecv.at[s], me, other).wait_recv()
+        return carry
+
+    lax.fori_loop(0, n, finish, 0)
+
+    def drain(h, carry):
+        sends(h, True)
+        return carry
+
+    lax.fori_loop(0, heads, drain, 0)
+
+
+def project(tokens, gain, w_qkv, n):
+    rows, feats = tokens.shape
+    heads = w_qkv.shape[2] // HEAD_DIM
+    half = rows // 2
+    bf = jnp.bfloat16
+    dma = pltpu.SemaphoreType.DMA
+    return pl.pallas_call(
+        functools.partial(project_kernel, n, heads),
+        out_shape=(
+            jax.ShapeDtypeStruct((n, half, HEAD_DIM), bf),
+            jax.ShapeDtypeStruct((2, n, half, 2 * HEAD_DIM), bf),
+        ),
+        in_specs=[ANY, pl.BlockSpec(memory_space=pltpu.VMEM), ANY],
+        out_specs=(ANY, ANY),
+        scratch_shapes=[
+            pltpu.VMEM((2, rows, feats), bf),
+            pltpu.VMEM((rows, 2 * feats), bf),
+            pltpu.VMEM((heads // 2, 3, 2 * feats, 2 * HEAD_DIM), bf),
+            pltpu.VMEM((heads, rows, HEAD_DIM), bf),
+            pltpu.VMEM((heads, rows, 2 * HEAD_DIM), bf),
+            dma((heads // 2, 3)), dma((3,)), dma((heads, 2)), dma((heads, 2)),
+            dma((n,)), dma((n,)), dma((n,)), dma((n,)),
+        ],
+        compiler_params=pltpu.CompilerParams(has_side_effects=True, vmem_limit_bytes=48 * 1024 * 1024),
+        name="project",
+    )(tokens, gain, w_qkv)
+
+
+def attend_kernel(chunk, group, q_ref, kv_ref, out_ref, vones):
+    keys = kv_ref.shape[0]
+
+    @pl.when(pl.program_id(0) == 0)
+    def _():
+        vones[:, :HEAD_DIM] = kv_ref[:, HEAD_DIM:]
+        vones[:, HEAD_DIM:] = jnp.ones((keys, HEAD_DIM), jnp.bfloat16)
+
+    parts = q_ref.shape[0] // group
+    queries = [q_ref[g * group : (g + 1) * group, :] for g in range(parts)]
+
+    def body(i, carry):
+        at = pl.ds(pl.multiple_of(i * chunk, chunk), chunk)
+        kept = []
+        scores = [
+            lax.dot_general(q, kv_ref[at, :HEAD_DIM], (((1,), (1,)), ((), ())), preferred_element_type=jnp.float32)
+            for q in queries
+        ]
+        for (top, total), s in zip(carry, scores):
+            high = jnp.maximum(top, jnp.max(s, axis=1, keepdims=True))
+            p = jnp.exp2((s - high).astype(jnp.bfloat16))
+            add = jnp.dot(p, vones[at, :], preferred_element_type=jnp.float32)
+            kept.append((high, total * jnp.exp2(top - high) + add))
+        return tuple(kept)
+
+    start = tuple(
+        (jnp.full((group, 1), -1e30, jnp.float32), jnp.zeros((group, 2 * HEAD_DIM), jnp.float32)) for _ in queries
+    )
+    done = lax.fori_loop(0, keys // chunk, body, start, unroll=2)
+    for g, (_, total) in enumerate(done):
+        out_ref[g * group : (g + 1) * group, :] = (total[:, :HEAD_DIM] / total[:, HEAD_DIM:]).astype(jnp.bfloat16)
+
+
+def attend(q, kv, block=512, group=256, chunk=1024):
+    count, keys = q.shape[0], kv.shape[0]
+    block = math.gcd(block, count)
+    group = math.gcd(group, block)
+    chunk = math.gcd(chunk, keys)
+    return pl.pallas_call(
+        functools.partial(attend_kernel, chunk, group),
+        grid=(count // block,),
+        out_shape=jax.ShapeDtypeStruct((count, HEAD_DIM), jnp.bfloat16),
+        in_specs=[
+            pl.BlockSpec((block, HEAD_DIM), lambda i: (i, 0)),
+            pl.BlockSpec((keys, 2 * HEAD_DIM), lambda i: (0, 0)),
+        ],
+        out_specs=pl.BlockSpec((block, HEAD_DIM), lambda i: (i, 0)),
+        scratch_shapes=[pltpu.VMEM((keys, 2 * HEAD_DIM), jnp.bfloat16)],
+        compiler_params=pltpu.CompilerParams(
+            dimension_semantics=("arbitrary",), vmem_limit_bytes=48 * 1024 * 1024
+        ),
+        name="attend",
+    )(q, kv)
+
+
+def output_kernel(n, heads, ctx, tok, w, out, held, sent, came, send, recv, psem):
+    me, core = lax.axis_index("seq"), lax.axis_index("tp")
+    other = 1 - core
+    rows, feats = tok.shape
+    half = rows // 2
+    home, slot = me // heads, lax.rem(me, heads)
+
+    def place(u, h):
+        return held.at[
+            pl.ds(pl.multiple_of(u * half, half), half), pl.ds(pl.multiple_of(h * HEAD_DIM, HEAD_DIM), HEAD_DIM)
+        ]
+
+    def give(i, wait):
+        s = lax.rem(me + i, n)
+        own = jnp.logical_and(s == me, home == core)
+        args = (ctx.at[s], place(core, slot), send.at[s], recv.at[core, slot], s, home)
+        if wait:
+
+            @pl.when(jnp.logical_not(own))
+            def _():
+                remote(*args).wait_send()
+        else:
+            put(*args, own)
+
+    def start(i, carry):
+        give(i, False)
+        return carry
+
+    lax.fori_loop(0, n, start, 0)
+
+    def arrive(i, carry):
+        u, h = i // heads, lax.rem(i, heads)
+        remote(ctx.at[0], place(u, h), send.at[0], recv.at[u, h], me, other).wait_recv()
+        return carry
+
+    lax.fori_loop(0, 2 * heads, arrive, 0)
+
+    width = 2 * HEAD_DIM
+
+    def product(side, i):
+        at = pl.ds(pl.multiple_of(side * feats + i * width, width), width)
+        return jnp.dot(held[...], w[:, at], preferred_element_type=jnp.float32)
+
+    pieces = feats // width
+
+    def share(i):
+        return remote(sent.at[i], came.at[i], psem.at[0, i], psem.at[1, i], me, other)
+
+    def theirs(i, carry):
+        sent[i] = product(other, i).astype(jnp.bfloat16)
+
+        @pl.when(i > 0)
+        def _():
+            share(i - 1).start()
+
+        return carry
+
+    lax.fori_loop(0, pieces, theirs, 0)
+    share(pieces - 1).start()
+
+    def ours(i, carry):
+        at = pl.ds(pl.multiple_of(i * width, width), width)
+        got = product(core, i)
+        share(i).wait_recv()
+        out[:, at] = (tok[:, at].astype(jnp.float32) + (got + came[i].astype(jnp.float32))).astype(jnp.bfloat16)
+        return carry
+
+    lax.fori_loop(0, pieces, ours, 0)
+
+    def drain(i, carry):
+        give(i, True)
+        return carry
+
+    lax.fori_loop(0, n, drain, 0)
+    for i in range(pieces):
+        share(i).wait_send()
+
+
+def output(ctx, tokens, w_out, n):
+    rows, feats = tokens.shape
+    heads = w_out.shape[0] // HEAD_DIM
+    bf = jnp.bfloat16
+    dma = pltpu.SemaphoreType.DMA
+    vm = pl.BlockSpec(memory_space=pltpu.VMEM)
+    pieces = feats // (2 * HEAD_DIM)
+    return pl.pallas_call(
+        functools.partial(output_kernel, n, heads),
+        out_shape=jax.ShapeDtypeStruct((rows, feats), bf),
+        in_specs=[ANY, vm, vm],
+        out_specs=vm,
+        scratch_shapes=[
+            pltpu.VMEM((rows, heads * HEAD_DIM), bf),
+            pltpu.VMEM((pieces, rows, 2 * HEAD_DIM), bf),
+            pltpu.VMEM((pieces, rows, 2 * HEAD_DIM), bf),
+            dma((n,)), dma((2, heads)), dma((2, pieces)),
+        ],
+        compiler_params=pltpu.CompilerParams(has_side_effects=True, vmem_limit_bytes=32 * 1024 * 1024),
+        name="output",
+    )(ctx, tokens, w_out)
+
+
+def head_per_chip(n, tokens, ln_gain, w_qkv, w_out):
+    gain = ln_gain.astype(jnp.float32).reshape(1, -1)
+    q, kv = project(tokens, gain, w_qkv, n)
+    half = q.shape[1]
+    ctx = attend(q.reshape(n * half, HEAD_DIM), kv.reshape(2 * n * half, 2 * HEAD_DIM))
+    return output(ctx.reshape(n, half, HEAD_DIM), tokens, w_out, n)
 
 
 def attend_block(totals, queries, block_kv, factor):
@@ -71,6 +402,12 @@
 def solution(mesh):
     in_specs = (P("seq", "tp"), P(), P(None, None, "tp"), P("tp", None))
     out_specs = P("seq", "tp")
-    return jax.shard_map(
-        on_device, mesh=mesh, in_specs=in_specs, out_specs=out_specs, check_vma=False
-    )
+    n, cores = mesh.shape["seq"], mesh.shape["tp"]
+
+    def run(tokens, ln_gain, w_qkv, w_out):
+        heads = w_qkv.shape[2] // HEAD_DIM
+        if cores == 2 and heads * cores == n and heads % 2 == 0:
+            return head_per_chip(n, tokens, ln_gain, w_qkv, w_out)
+        return on_device(tokens, ln_gain, w_qkv, w_out)
+
+    return jax.shard_map(run, mesh=mesh, in_specs=in_specs, out_specs=out_specs, check_vma=False)

time: 601 us -> 204 us (0.34)
  waiting for transfers between devices: 373 us -> 0 us
  Pallas kernels: 0 us -> 201 us
  matrix products: 115 us -> 0 us
  local copies, waits for them, and re-layouts: 50.9 us -> 2.21 us
  other arithmetic: 47 us -> 0.69 us
  between operations: 13.2 us -> 0.06 us
    all_gather x2 -> x0, waiting for transfers between devices: 360 us -> none  [the longest x1 347 us: on_device(): lax.all_gather(keys_vals, 'seq', axis=1, tiled=True)]
    pallas_call x0 -> x3, Pallas kernels: none -> 201 us  [the longest x1 106 us: project(): pl.pallas_call(functools.partial(project_kernel, n, heads), out_shape=(ja...]
    dot_general x4 -> x0, matrix products: 115 us -> none  [the longest x1 50.1 us: attend_block(): jnp.einsum('thc,shc->ths', queries, keys_part, preferred_element_type=jnp...]
    reduce_sum x2 -> x0, other arithmetic: 43.7 us -> none  [the longest x1 41.4 us: attend_block(): denoms = jnp.sum(expon, axis=2)]
    unnamed x6 -> x7, local copies, waits for them, and re-layouts: 28.7 us -> 2.21 us
    another operation x1 -> x0, local copies, waits for them, and re-layouts: 20.7 us -> none  [attend_block(): block_kv[1].reshape(block_kv.shape[1], heads_here, queries.shape[2])]
    reduce_scatter x1 -> x0, waiting for transfers between devices: 12.1 us -> none  [on_device(): lax.psum_scatter(lax.dot_general(w_out, context, (((0,), (1,)), ((), ()))...]
  transfers between devices with their start and end apart: 3 -> 0, of which waited for: 3 -> 0; matrix products, arithmetic and copies ran while one was open for 0% -> 0% of each run, Pallas kernels for 0% -> 0%
where the time goes in v1:
time: 204 us
  Pallas kernels  201 us (99%)
  local copies, waits for them, and re-layouts  2.21 us (1%)
    pallas_call x1, Pallas kernels, project(): pl.pallas_call(functools.partial(project_kernel, n, heads), out_shape=(ja...  106 us
    pallas_call x1, Pallas kernels, attend(): pl.pallas_call(functools.partial(attend_kernel, chunk, group), grid=(coun...  59.9 us
    pallas_call x1, Pallas kernels, output(): pl.pallas_call(functools.partial(output_kernel, n, heads), out_shape=jax....  34.9 us

profile of v1, /device:TPU:15, one launch (start us, length us, event | category | flops | bytes accessed | tf_op | source)
XLA Modules:
  0.0 203.8 jit_solution(1093976069929413389)
XLA Ops:
  0.0 0.7 reshape.19
  0.7 0.0 copy-start
  0.7 1.2 copy-done
  1.9 106.1 %project.1 = (bf16[16,256,128]{2,1,0:T(8,128)(2,1)S(1)}, bf16[2,16,256,256]{3,2,1,0:T(8,128)(2,1)}) custom-call(bf16[512,1024]{1,0:T(8,128)(2,1)S(1)} %copy-done, f32[1,2048]{1,0:T(1,128)S(1)} %bitcast.6, bf16[3,2048,1024]{2,1,0:T(8,128)(2,1)} %w.2), custom_call_target="tpu_custom_call" | custom-call | tf_op jit(solution)/shard_map/project/pallas_call | solution.py:154
  108.0 0.0 copy-start.1
  108.0 0.0 copy-start.2
  108.0 59.9 %attend.1 = bf16[4096,128]{1,0:T(8,128)(2,1)S(1)} custom-call(bf16[4096,128]{1,0:T(8,128)(2,1)S(1)} %bitcast.5, bf16[8192,256]{1,0:T(8,128)(2,1)} %bitcast.7), custom_call_target="tpu_custom_call" | custom-call | tf_op jit(solution)/shard_map/attend/pallas_call | solution.py:214
  167.9 0.0 copy-done.1
  167.9 0.0 copy-done.2
  167.9 34.9 %output.1 = bf16[512,1024]{1,0:T(8,128)(2,1)S(1)} custom-call(bf16[16,256,128]{2,1,0:T(8,128)(2,1)S(1)} %bitcast.4, bf16[512,1024]{1,0:T(8,128)(2,1)S(1)} %copy-done.1, bf16[1024,2048]{1,0:T(8,128)(2,1)S(1)} %copy-done.2), custom_call_target="tpu_custom_call" | custom-call | tf_op jit(solution)/shard_map/output/pallas_call | solution.py:316
  202.9 1.0 copy.6
Async XLA Ops:
  0.7 1.2 copy-start
  108.0 59.9 %copy-start.1 = (bf16[512,1024]{1,0:T(8,128)(2,1)S(1)}, bf16[512,1024]{1,0:T(8,128)(2,1)}, u32[]{:S(2)}) copy-start(bf16[512,1024]{1,0:T(8,128)(2,1)} %tok.3) | copy-start | bytes 3145732
  108.0 59.9 %copy-start.2 = (bf16[1024,2048]{1,0:T(8,128)(2,1)S(1)}, bf16[1024,2048]{1,0:T(8,128)(2,1)}, u32[]{:S(2)}) copy-start(bf16[1024,2048]{1,0:T(8,128)(2,1)} %w.3) | copy-start | bytes 12582916
